TPU v7x, 32 devices: a whole 2x2x4 slice. The times are simulated.
32 devices in a mesh: head: 4 (over x, core), outer: 2 (over y), inner: 4 (over z).
Axes of the slice: x: 2, y: 2, z: 4, core: 2. Of those that a mesh axis runs over, the one named last changes fastest.
Arguments:
- queries: bfloat16 [8, 256, 4096], P(('outer', 'inner'), 'head'), may hold values from -120 to 120
- keys: bfloat16 [8, 256, 1024], P(('outer', 'inner'), 'head'), may hold values from -6 to 6
- values: bfloat16 [8, 256, 1024], P(('outer', 'inner'), 'head'), may hold values from -6 to 6
- doc_lengths: int32 [4], replicated, may hold values from 1 to 1024, 2048 in all
Outputs:
- attended: bfloat16 [8, 256, 4096], P(('outer', 'inner'), 'head')
Inputs may be any that keep to these rules, and one draw needn't show every extreme that they name: `doc_lengths`: the documents of the packed sequence in order, summing to 2048.
All inputs are finite; a program needn't handle non-finite values.
Results may differ from a plain program's by a relative error of at most 0.0044.
Values may be sent and summed in bfloat16 or wider, within the bound.
A program may use at most 64 MiB of HBM per device.

v0:
```python
import math
import jax
import jax.numpy as jnp
from jax import lax
from jax.sharding import PartitionSpec as P

HD = 128
MAXDOC = 4096
NEG_FILL = -1e30


def passed_along(block, axis, distance):
    devices = range(lax.axis_size(axis))
    route = [(i - distance, i) for i in devices if i - distance in devices]
    return lax.ppermute(block, axis, route)


def doc_index(positions, doc_lengths):
    ends = jnp.cumsum(doc_lengths)
    return jnp.sum((positions[:, None] >= ends[None, :]).astype(jnp.int32), axis=1)


def fold_block(state, key_block, value_block, offset, context):
    q_heads, q_pos, q_doc, rank, doc_lengths = context
    rows = key_block.shape[0]
    heads = key_block.shape[1] // HD
    k_pos = (rank - offset) * rows + jnp.arange(rows, dtype=jnp.int32)
    k_doc = doc_index(k_pos, doc_lengths)
    visible = (
        (k_pos[None, :] >= 0)
        & (k_pos[None, :] <= q_pos[:, None])
        & (k_doc[None, :] == q_doc[:, None])
    )
    k_heads = key_block.reshape(rows, heads, HD)
    v_heads = value_block.reshape(rows, heads, HD)
    scores = jnp.einsum("qgeh,kgh->geqk", q_heads, k_heads, preferred_element_type=jnp.float32) * (
        1.0 / math.sqrt(HD)
    )
    running, total, summed = state
    masked = jnp.where(visible[None, None], scores, NEG_FILL)
    peak = jnp.maximum(running, jnp.max(masked, axis=-1))
    factor = jnp.exp(running - peak)
    weights = jnp.where(visible[None, None], jnp.exp(scores - peak[..., None]), 0.0)
    total = total * factor + jnp.sum(weights, axis=-1)
    rounded = weights.astype(jnp.bfloat16)
    added = jnp.einsum("geqk,kgh->qgeh", rounded, v_heads, preferred_element_type=jnp.float32)
    summed = summed * jnp.transpose(factor, (2, 0, 1))[..., None] + added
    return (peak, total, summed)


def body(queries, keys, values, doc_lengths):
    q_local, k_local, v_local = (
        lax.all_to_all(queries, "head", split_axis=2, concat_axis=1, tiled=True),
        lax.all_to_all(keys, "head", split_axis=2, concat_axis=1, tiled=True),
        lax.all_to_all(values, "head", split_axis=2, concat_axis=1, tiled=True),
    )
    rows = q_local.shape[1]
    kv_heads = k_local.shape[2] // HD
    group = q_local.shape[2] // k_local.shape[2]
    q_heads = q_local[0].reshape(rows, kv_heads, group, HD)
    rank = lax.axis_index(("outer", "inner"))
    reach = min(MAXDOC // rows, lax.axis_size(("outer", "inner")) // 2)
    q_pos = rank * rows + jnp.arange(rows, dtype=jnp.int32)
    q_doc = doc_index(q_pos, doc_lengths)
    context = (q_heads, q_pos, q_doc, rank, doc_lengths)
    state = (
        jnp.full((kv_heads, group, rows), NEG_FILL, jnp.float32),
        jnp.zeros((kv_heads, group, rows), jnp.float32),
        jnp.zeros((rows, kv_heads, group, HD), jnp.float32),
    )

    def attend(state, key_block, value_block, offset):
        return fold_block(state, key_block, value_block, offset, context)

    state = attend(state, k_local[0], v_local[0], 0)
    key_window = k_local
    value_window = v_local
    held = 1
    while held < reach + 1:
        extra = min(held, reach + 1 - held)
        sent_keys, sent_values = passed_along(
            (key_window[held - extra :], value_window[held - extra :]), ("outer", "inner"), held
        )
        key_window = jnp.concatenate([sent_keys, key_window], axis=0)
        value_window = jnp.concatenate([sent_values, value_window], axis=0)
        held = held + extra

    def sweep(offset, carried):
        index = reach - offset
        key_block = lax.dynamic_index_in_dim(key_window, index, 0, keepdims=False)
        value_block = lax.dynamic_index_in_dim(value_window, index, 0, keepdims=False)
        return attend(carried, key_block, value_block, offset)

    state = lax.fori_loop(1, reach + 1, sweep, state)
    running, total, summed = state
    result = summed / jnp.transpose(total, (2, 0, 1))[..., None]
    attended = result.astype(jnp.bfloat16).reshape(1, rows, kv_heads * group * HD)
    return lax.all_to_all(attended, "head", split_axis=1, concat_axis=2, tiled=True)


def solution(mesh):
    placed = (
        P(("outer", "inner"), "head", None),
        P(("outer", "inner"), "head", None),
        P(("outer", "inner"), "head", None),
        P(),
    )
    return jax.shard_map(
        body,
        mesh=mesh,
        in_specs=placed,
        out_specs=P(("outer", "inner"), "head", None),
        check_vma=False,
    )
```

profile of v0, /device:TPU:4, one launch (start us, length us, event | category | flops | bytes accessed | tf_op | source)
XLA Modules:
  0.0 129.2 jit_solution(5051317125559907742)
XLA Ops:
  0.0 1.3 copy.102
  1.3 0.5 broadcast.232
  1.8 2.2 %reduce.1 = bf16[1024,64]{1,0:T(8,128)(2,1)S(1)} reduce(bf16[1024,1,64]{2,1,0:T(2,128)(2,1)S(1)} %bitcast.132, bf16[]{:T(256)} %broadcast.232), dimensions={1}, to_apply=%bitcast.73.reduce_sub_computation | reduce | bytes 262146
  4.0 0.9 reshape.228
  4.9 3.3 %all-to-all-start = ((bf16[4,2,8192]{2,1,0:T(2,128)(2,1)}), bf16[4,2,8192]{2,1,0:T(2,128)(2,1)S(1)}, u32[]{:S(2)}, u32[]{:S(2)}) async-start(bf16[4,2,8192]{2,1,0:T(2,128)(2,1)} %reshape.228), calls=%async_computation | async-start | bytes 262144 | tf_op jit(solution)/shard_map/all_to_all | solution.py:54
  8.3 2.8 %copy.105 = bf16[1,64,4096]{1,0,2:T(2,128)(2,1)S(1)} copy(bf16[1,64,4096]{2,1,0:T(8,128)(2,1)S(1)} %copy-done) | data formatting | bytes 1048576 | tf_op args[0]
  11.1 22.4 %reduce = bf16[4096,64]{1,0:T(8,128)(2,1)S(1)} reduce(bf16[4096,1,64]{2,1,0:T(2,128)(2,1)S(1)} %bitcast.124, bf16[]{:T(256)} %broadcast.232), dimensions={1}, to_apply=%bitcast.75.reduce_sub_computation | reduce | bytes 1048578
  33.5 1.6 %reshape.230 = bf16[4,2,32768]{2,1,0:T(2,128)(2,1)} reshape(bf16[4096,64]{1,0:T(8,128)(2,1)S(1)} %reduce) | data formatting | bytes 1048576
  35.1 0.4 copy.110
  35.5 2.2 %reduce.2 = bf16[1024,64]{1,0:T(8,128)(2,1)S(1)} reduce(bf16[1024,1,64]{2,1,0:T(2,128)(2,1)S(1)} %bitcast.133, bf16[]{:T(256)} %broadcast.232), dimensions={1}, to_apply=%bitcast.77.reduce_sub_computation | reduce | bytes 262146
  37.7 0.9 reshape.232
  38.6 0.2 broadcast_in_dim.114
  38.9 3.3 %all-to-all-start.2 = ((bf16[4,2,8192]{2,1,0:T(2,128)(2,1)}), bf16[4,2,8192]{2,1,0:T(2,128)(2,1)S(1)}, u32[]{:S(2)}, u32[]{:S(2)}) async-start(bf16[4,2,8192]{2,1,0:T(2,128)(2,1)} %reshape.232), calls=%async_computation.2 | async-start | bytes 262144 | tf_op jit(solution)/shard_map/all_to_all | solution.py:55
  42.2 0.3 reshape.229
  42.6 0.3 copy.103
  43.0 3.8 %all-to-all-done.2 = bf16[4,2,8192]{2,1,0:T(2,128)(2,1)S(1)} async-done(((bf16[4,2,8192]{2,1,0:T(2,128)(2,1)}), bf16[4,2,8192]{2,1,0:T(2,128)(2,1)S(1)}, u32[]{:S(2)}, u32[]{:S(2)}) %all-to-all-start.2) | async-done | bytes 131104 | tf_op jit(solution)/shard_map/all_to_all | solution.py:55
  46.8 3.5 %all-to-all-start.1 = ((bf16[4,2,32768]{2,1,0:T(2,128)(2,1)}), bf16[4,2,32768]{2,1,0:T(2,128)(2,1)S(1)}, u32[]{:S(2)}, u32[]{:S(2)}) async-start(bf16[4,2,32768]{2,1,0:T(2,128)(2,1)} %reshape.230), calls=%async_computation.1 | async-start | bytes 1048576 | tf_op jit(solution)/shard_map/all_to_all | solution.py:53
  50.2 0.3 reshape.233
  50.6 0.3 copy.111
  51.0 3.5 %collective-permute-start.1 = (bf16[1,256,256]{2,1,0:T(8,128)(2,1)S(1)}, bf16[1,256,256]{2,1,0:T(8,128)(2,1)S(1)}, u32[]{:S(2)}, u32[]{:S(2)}) collective-permute-start(bf16[1,256,256]{2,1,0:T(8,128)(2,1)S(1)} %bitcast.135), channel_id=1, source_target_pairs={{0,1},{1,2},{2,3},{3,4},{4,5},{5,6},{6,7},{8,9},{9,10},{10,11},{11... | collective-permute-start | bytes 393224 | tf_op jit(solution)/shard_map/ppermute | solution.py:15
  54.5 3.5 %collective-permute-start.4 = (bf16[1,256,256]{2,1,0:T(8,128)(2,1)S(1)}, bf16[1,256,256]{2,1,0:T(8,128)(2,1)S(1)}, u32[]{:S(2)}, u32[]{:S(2)}) collective-permute-start(bf16[1,256,256]{2,1,0:T(8,128)(2,1)S(1)} %bitcast.139), channel_id=1, source_target_pairs={{0,1},{1,2},{2,3},{3,4},{4,5},{5,6},{6,7},{8,9},{9,10},{10,11},{11... | collective-permute-start | bytes 393224 | tf_op jit(solution)/shard_map/ppermute | solution.py:15
  58.2 0.7 reshape_squeeze.11
  58.9 1.3 collective-permute-start
  60.2 1.3 %collective-permute-start.3 = (bf16[1,256,256]{2,1,0:T(8,128)(2,1)S(1)}, bf16[1,256,256]{2,1,0:T(8,128)(2,1)S(1)}, u32[]{:S(2)}, u32[]{:S(2)}) collective-permute-start(bf16[1,256,256]{2,1,0:T(8,128)(2,1)S(1)} %bitcast.140), channel_id=1, source_target_pairs={{0,4},{1,5},{2,6},{3,7},{8,12},{9,13},{10,14},{11,15},{16,20},{17,... | collective-permute-start | bytes 393224 | tf_op jit(solution)/shard_map/ppermute | solution.py:15
  61.5 0.7 pad_maximum_fusion.2
  62.2 3.1 %collective-permute-start.2 = (bf16[2,256,256]{2,1,0:T(8,128)(2,1)}, bf16[2,256,256]{2,1,0:T(8,128)(2,1)}, u32[]{:S(2)}, u32[]{:S(2)}) collective-permute-start(bf16[2,256,256]{2,1,0:T(8,128)(2,1)} %pad_maximum_fusion.2), channel_id=1, source_target_pairs={{0,2},{1,3},{2,4},{3,5},{4,6},{5,7},{8,10},{9,11},{10,12},{11,13},... | collective-permute-start | bytes 786440 | tf_op jit(solution)/shard_map/ppermute | solution.py:15
  65.4 0.7 pad_maximum_fusion.3
  66.1 1.9 %collective-permute-start.5 = (bf16[2,256,256]{2,1,0:T(8,128)(2,1)}, bf16[2,256,256]{2,1,0:T(8,128)(2,1)}, u32[]{:S(2)}, u32[]{:S(2)}) collective-permute-start(bf16[2,256,256]{2,1,0:T(8,128)(2,1)} %pad_maximum_fusion.3), channel_id=1, source_target_pairs={{0,2},{1,3},{2,4},{3,5},{4,6},{5,7},{8,10},{9,11},{10,12},{11,13},... | collective-permute-start | bytes 786440 | tf_op jit(solution)/shard_map/ppermute | solution.py:15
  68.0 0.9 reshape.231
  68.9 2.3 %copy.106 = bf16[1,64,4096]{2,1,0:T(8,128)(2,1)S(1)} copy(bf16[1,64,4096]{1,0,2:T(2,128)(2,1)S(1)} %bitcast.123) | data formatting | bytes 1048576 | tf_op jit(solution)/shard_map/all_to_all | solution.py:53
  71.2 0.4 all_to_all.54
  71.7 0.4 reshape_squeeze.10
  72.1 0.5 fusion.16
  72.6 0.5 fusion.20
  73.1 0.8 fusion.21
  74.0 0.9 copy.109
  74.9 0.3 copy.117
  75.2 11.6 %collective-permute-done.2 = bf16[2,256,256]{2,1,0:T(8,128)(2,1)} collective-permute-done((bf16[2,256,256]{2,1,0:T(8,128)(2,1)}, bf16[2,256,256]{2,1,0:T(8,128)(2,1)}, u32[]{:S(2)}, u32[]{:S(2)}) %collective-permute-start.2) | collective-permute-done | bytes 262176 | tf_op jit(solution)/shard_map/ppermute | solution.py:15
  86.8 1.9 %pad_maximum_fusion = bf16[5,256,256]{2,1,0:T(8,128)(2,1)} fusion(bf16[1,256,256]{2,1,0:T(8,128)(2,1)S(1)} %bitcast.138, bf16[1,256,256]{2,1,0:T(8,128)(2,1)S(1)} %collective-permute-done.1, bf16[2,256,256]{2,1,0:T(8,128)(2,1)} %collective-permute-done.2, bf16[1,256,256]{2,1,0:T(8,128)(2,1)} %collective-permute-done), kind=kLoop, calls=%fused_computation.40 | loop fusion | flops 983040 | bytes 1310720 | tf_op jit(solution)/shard_map/concatenate | solution.py:84
  88.7 2.9 %collective-permute-done.5 = bf16[2,256,256]{2,1,0:T(8,128)(2,1)} collective-permute-done((bf16[2,256,256]{2,1,0:T(8,128)(2,1)}, bf16[2,256,256]{2,1,0:T(8,128)(2,1)}, u32[]{:S(2)}, u32[]{:S(2)}) %collective-permute-start.5) | collective-permute-done | bytes 262176 | tf_op jit(solution)/shard_map/ppermute | solution.py:15
  91.6 1.9 %pad_maximum_fusion.1 = bf16[5,256,256]{2,1,0:T(8,128)(2,1)} fusion(bf16[1,256,256]{2,1,0:T(8,128)(2,1)S(1)} %bitcast.142, bf16[1,256,256]{2,1,0:T(8,128)(2,1)S(1)} %collective-permute-done.4, bf16[2,256,256]{2,1,0:T(8,128)(2,1)} %collective-permute-done.5, bf16[1,256,256]{2,1,0:T(8,128)(2,1)S(1)} %collective-permute-done.3), kind=kLoop, calls=%fused_computation.41 | loop fusion | flops 983040 | bytes 1310720 | tf_op jit(solution)/shard_map/concatenate | solution.py:85
  93.5 17.5 %while.20 = (s32[]{:T(128)}, f32[2,4,256]{2,1,0:T(4,128)S(1)}, f32[2,4,256]{2,1,0:T(4,128)S(1)}, f32[256,2,4,128]{0,3,2,1:T(8,128)S(1)}, s32[]{:T(128)}, /*index...) while((s32[]{:T(128)}, f32[2,4,256]{2,1,0:T(4,128)S(1)}, ...), condition=%wide.region_8.9_spmd.clone, body=%wide.region_4.0_spmd.clone.sunk | while | flops 274999040 | bytes 10625787 | solution.py:94
  93.8 1.0 constant_dynamic-slice_fusion.3
  94.9 1.6 %fusion.50 = (f32[2,4,256]{2,1,0:T(4,128)S(1)}, f32[2,256,256,4]{2,1,3,0:T(8,128)S(1)}) fusion(pred[256,256]{0,1:T(8,128)(4,1)S(1)} %compare_and_fusion.3, bf16[256,2,128,1]{0,2,3,1:T(8,128)(2,1)S(1)} %bitcast.121, bf16[256,2,4,128]{3,0,2,1:T(8,128)(2,1)} %get-tuple-element.533), kind=kOutput, calls=%fused_computation.3.clone.1 | convolution fusion | flops 135788544 | bytes 2826240 | tf_op jit(solution)/shard_map/while/body/eval_jaxpr/qgeh,kgh->geqk/dot_general | solution.py:36
  96.6 0.8 fusion.53
  97.3 0.5 fusion.52
  98.1 1.0 constant_dynamic-slice_fusion.3
  99.2 1.6 %fusion.50 = (f32[2,4,256]{2,1,0:T(4,128)S(1)}, f32[2,256,256,4]{2,1,3,0:T(8,128)S(1)}) fusion(pred[256,256]{0,1:T(8,128)(4,1)S(1)} %compare_and_fusion.3, bf16[256,2,128,1]{0,2,3,1:T(8,128)(2,1)S(1)} %bitcast.121, bf16[256,2,4,128]{3,0,2,1:T(8,128)(2,1)} %get-tuple-element.533), kind=kOutput, calls=%fused_computation.3.clone.1 | convolution fusion | flops 135788544 | bytes 2826240 | tf_op jit(solution)/shard_map/while/body/eval_jaxpr/qgeh,kgh->geqk/dot_general | solution.py:36
  101.0 0.8 fusion.53
  101.7 0.5 fusion.52
  102.5 1.0 constant_dynamic-slice_fusion.3
  103.6 1.6 %fusion.50 = (f32[2,4,256]{2,1,0:T(4,128)S(1)}, f32[2,256,256,4]{2,1,3,0:T(8,128)S(1)}) fusion(pred[256,256]{0,1:T(8,128)(4,1)S(1)} %compare_and_fusion.3, bf16[256,2,128,1]{0,2,3,1:T(8,128)(2,1)S(1)} %bitcast.121, bf16[256,2,4,128]{3,0,2,1:T(8,128)(2,1)} %get-tuple-element.533), kind=kOutput, calls=%fused_computation.3.clone.1 | convolution fusion | flops 135788544 | bytes 2826240 | tf_op jit(solution)/shard_map/while/body/eval_jaxpr/qgeh,kgh->geqk/dot_general | solution.py:36
  105.3 0.8 fusion.53
  106.1 0.5 fusion.52
  106.9 1.0 constant_dynamic-slice_fusion.3
  108.0 1.6 %fusion.50 = (f32[2,4,256]{2,1,0:T(4,128)S(1)}, f32[2,256,256,4]{2,1,3,0:T(8,128)S(1)}) fusion(pred[256,256]{0,1:T(8,128)(4,1)S(1)} %compare_and_fusion.3, bf16[256,2,128,1]{0,2,3,1:T(8,128)(2,1)S(1)} %bitcast.121, bf16[256,2,4,128]{3,0,2,1:T(8,128)(2,1)} %get-tuple-element.533), kind=kOutput, calls=%fused_computation.3.clone.1 | convolution fusion | flops 135788544 | bytes 2826240 | tf_op jit(solution)/shard_map/while/body/eval_jaxpr/qgeh,kgh->geqk/dot_general | solution.py:36
  109.7 0.8 fusion.53
  110.5 0.5 fusion.52
  111.1 1.0 copy.121
  112.1 3.7 %reduce.3 = bf16[256,1024]{1,0:T(8,128)(2,1)S(1)} reduce(bf16[256,1,1024]{2,1,0:T(2,128)(2,1)S(1)} %bitcast.127, bf16[]{:T(256)} %broadcast.232), dimensions={1}, to_apply=%bitcast.79.reduce_sub_computation | reduce | bytes 1048578
  115.7 0.4 reshape.234
  116.1 11.5 %all_to_all.69 = bf16[4,2,32768]{2,1,0:T(2,128)(2,1)S(1)} all-to-all(bf16[4,2,32768]{2,1,0:T(2,128)(2,1)S(1)} %reshape.234), channel_id=1, replica_groups=mesh['head'=4,'outer'=2,'inner'=4] {'head'}, dimensions={0} | all-to-all | bytes 1048576 | tf_op jit(solution)/shard_map/all_to_all | solution.py:98
  127.6 0.5 reshape.235
  128.3 0.8 copy.138
  (64 shorter events, 2.9 us)
Async XLA Ops:
  0.0 8.3 %copy-start = (bf16[1,64,4096]{2,1,0:T(8,128)(2,1)S(1)}, bf16[1,64,4096]{2,1,0:T(8,128)(2,1)}, u32[]{:S(2)}) copy-start(bf16[1,64,4096]{2,1,0:T(8,128)(2,1)} %param.6) | copy-start | bytes 1572868
  4.9 33.9 %all-to-all-start = ((bf16[4,2,8192]{2,1,0:T(2,128)(2,1)}), bf16[4,2,8192]{2,1,0:T(2,128)(2,1)S(1)}, u32[]{:S(2)}, u32[]{:S(2)}) async-start(bf16[4,2,8192]{2,1,0:T(2,128)(2,1)} %reshape.228), calls=%async_computation | async-start | bytes 262144 | tf_op jit(solution)/shard_map/all_to_all | solution.py:54
  11.1 24.0 %copy-start.1 = (bf16[1,64,1024]{2,1,0:T(8,128)(2,1)S(1)}, bf16[1,64,1024]{2,1,0:T(8,128)(2,1)}, u32[]{:S(2)}) copy-start(bf16[1,64,1024]{2,1,0:T(8,128)(2,1)} %param.8) | copy-start | bytes 393220
  33.5 5.1 %copy-start.3 = (s32[4]{0:T(128)S(1)}, s32[4]{0:T(128)}, u32[]{:S(2)}) copy-start(s32[4]{0:T(128)} %param.9) | copy-start | bytes 52
  38.9 7.9 %all-to-all-start.2 = ((bf16[4,2,8192]{2,1,0:T(2,128)(2,1)}), bf16[4,2,8192]{2,1,0:T(2,128)(2,1)S(1)}, u32[]{:S(2)}, u32[]{:S(2)}) async-start(bf16[4,2,8192]{2,1,0:T(2,128)(2,1)} %reshape.232), calls=%async_computation.2 | async-start | bytes 262144 | tf_op jit(solution)/shard_map/all_to_all | solution.py:55
  46.8 21.2 %all-to-all-start.1 = ((bf16[4,2,32768]{2,1,0:T(2,128)(2,1)}), bf16[4,2,32768]{2,1,0:T(2,128)(2,1)S(1)}, u32[]{:S(2)}, u32[]{:S(2)}) async-start(bf16[4,2,32768]{2,1,0:T(2,128)(2,1)} %reshape.230), calls=%async_computation.1 | async-start | bytes 1048576 | tf_op jit(solution)/shard_map/all_to_all | solution.py:53
  51.0 10.5 %collective-permute-start.1 = (bf16[1,256,256]{2,1,0:T(8,128)(2,1)S(1)}, bf16[1,256,256]{2,1,0:T(8,128)(2,1)S(1)}, u32[]{:S(2)}, u32[]{:S(2)}) collective-permute-start(bf16[1,256,256]{2,1,0:T(8,128)(2,1)S(1)} %bitcast.135), channel_id=1, source_target_pairs={{0,1},{1,2},{2,3},{3,4},{4,5},{5,6},{6,7},{8,9},{9,10},{10,11},{11... | collective-permute-start | bytes 393224 | tf_op jit(solution)/shard_map/ppermute | solution.py:15
  54.5 10.8 %collective-permute-start.4 = (bf16[1,256,256]{2,1,0:T(8,128)(2,1)S(1)}, bf16[1,256,256]{2,1,0:T(8,128)(2,1)S(1)}, u32[]{:S(2)}, u32[]{:S(2)}) collective-permute-start(bf16[1,256,256]{2,1,0:T(8,128)(2,1)S(1)} %bitcast.139), channel_id=1, source_target_pairs={{0,1},{1,2},{2,3},{3,4},{4,5},{5,6},{6,7},{8,9},{9,10},{10,11},{11... | collective-permute-start | bytes 393224 | tf_op jit(solution)/shard_map/ppermute | solution.py:15
  58.9 16.3 %collective-permute-start = (bf16[1,256,256]{2,1,0:T(8,128)(2,1)S(1)}, bf16[1,256,256]{2,1,0:T(8,128)(2,1)}, u32[]{:S(2)}, u32[]{:S(2)}) collective-permute-start(bf16[1,256,256]{2,1,0:T(8,128)(2,1)S(1)} %bitcast.136), channel_id=1, source_target_pairs={{0,4},{1,5},{2,6},{3,7},{8,12},{9,13},{10,14},{11,15},{16,20},{17,... | collective-permute-start | bytes 393224 | tf_op jit(solution)/shard_map/ppermute | solution.py:15
  60.2 28.5 %collective-permute-start.3 = (bf16[1,256,256]{2,1,0:T(8,128)(2,1)S(1)}, bf16[1,256,256]{2,1,0:T(8,128)(2,1)S(1)}, u32[]{:S(2)}, u32[]{:S(2)}) collective-permute-start(bf16[1,256,256]{2,1,0:T(8,128)(2,1)S(1)} %bitcast.140), channel_id=1, source_target_pairs={{0,4},{1,5},{2,6},{3,7},{8,12},{9,13},{10,14},{11,15},{16,20},{17,... | collective-permute-start | bytes 393224 | tf_op jit(solution)/shard_map/ppermute | solution.py:15
  62.2 24.6 %collective-permute-start.2 = (bf16[2,256,256]{2,1,0:T(8,128)(2,1)}, bf16[2,256,256]{2,1,0:T(8,128)(2,1)}, u32[]{:S(2)}, u32[]{:S(2)}) collective-permute-start(bf16[2,256,256]{2,1,0:T(8,128)(2,1)} %pad_maximum_fusion.2), channel_id=1, source_target_pairs={{0,2},{1,3},{2,4},{3,5},{4,6},{5,7},{8,10},{9,11},{10,12},{11,13},... | collective-permute-start | bytes 786440 | tf_op jit(solution)/shard_map/ppermute | solution.py:15
  66.1 25.5 %collective-permute-start.5 = (bf16[2,256,256]{2,1,0:T(8,128)(2,1)}, bf16[2,256,256]{2,1,0:T(8,128)(2,1)}, u32[]{:S(2)}, u32[]{:S(2)}) collective-permute-start(bf16[2,256,256]{2,1,0:T(8,128)(2,1)} %pad_maximum_fusion.3), channel_id=1, source_target_pairs={{0,2},{1,3},{2,4},{3,5},{4,6},{5,7},{8,10},{9,11},{10,12},{11,13},... | collective-permute-start | bytes 786440 | tf_op jit(solution)/shard_map/ppermute | solution.py:15
  72.1 1.0 copy-start.2
where the time goes:
time: 130 us; the launch traced here: 129 us
  other arithmetic  39.8 us (31%)
  starting transfers between devices  24.7 us (19%)
  local copies, waits for them, and re-layouts  23.5 us (18%)
  waiting for transfers between devices  18.3 us (14%)
  blocking collectives  11.5 us (9%)
  matrix products  10.7 us (8%)
    unnamed x4, other arithmetic  30.5 us
    ppermute x6, starting transfers between devices, passed_along(): return lax.ppermute(block, axis, route)  14.6 us
    ppermute x6, waiting for transfers between devices, passed_along(): return lax.ppermute(block, axis, route)  14.5 us
    all_to_all x1, blocking collectives, body(): lax.all_to_all(attended, 'head', split_axis=1, concat_axis=2, tiled=True)  11.5 us
    unnamed x22, local copies, waits for them, and re-layouts  11.3 us
    dot_general x5, matrix products, fold_block(): jnp.einsum('qgeh,kgh->geqk', q_heads, k_heads, preferred_element_type=jnp...  6.84 us
    dynamic_slice x8, local copies, waits for them, and re-layouts, sweep(): lax.dynamic_index_in_dim(value_window, index, 0, keepdims=False)  4.36 us
    dot_general x5, matrix products, fold_block(): jnp.einsum('geqk,kgh->qgeh', rounded, v_heads, preferred_element_type=jnp...  3.91 us
  transfers between devices with their start and end apart: 9, of which 3 were waited for; matrix products, arithmetic and copies ran while one was open for 33% of the time, Pallas kernels for 0%

commit v1 on v0

--- a/solution.py
+++ b/solution.py
@@ -3,6 +3,7 @@
 import jax.numpy as jnp
 from jax import lax
 from jax.sharding import PartitionSpec as P
+from jax.lax import all_to_all, axis_size
 
 HD = 128
 MAXDOC = 4096
@@ -95,7 +96,16 @@
     running, total, summed = state
     result = summed / jnp.transpose(total, (2, 0, 1))[..., None]
     attended = result.astype(jnp.bfloat16).reshape(1, rows, kv_heads * group * HD)
-    return lax.all_to_all(attended, "head", split_axis=1, concat_axis=2, tiled=True)
+    prepare_point = lambda xs, dev_axis: jnp.concatenate(
+        all_to_all(
+            jnp.stack(jnp.split(xs, axis_size(dev_axis), axis=1), axis=0),
+            axis_name=dev_axis,
+            split_axis=0,
+            concat_axis=0,
+        ),
+        axis=2,
+    )
+    return prepare_point(attended, "head")
 
 
 def solution(mesh):

time: 130 us -> 125 us (0.962)
  other arithmetic: 39.8 us -> 36 us
  local copies, waits for them, and re-layouts: 23.5 us -> 22.1 us
    unnamed x4 -> x3, other arithmetic: 30.5 us -> 26.7 us
    unnamed x22 -> x23, local copies, waits for them, and re-layouts: 11.3 us -> 10.7 us
  transfers between devices with their start and end apart: 9 -> 9, of which waited for: 3 -> 3; matrix products, arithmetic and copies ran while one was open for 33% -> 34% of each run, Pallas kernels for 0% -> 0%
where the time goes in v1:
time: 125 us; the launch traced here: 124 us
  other arithmetic  36 us (29%)
  starting transfers between devices  24.7 us (20%)
  local copies, waits for them, and re-layouts  22.1 us (18%)
  waiting for transfers between devices  18.3 us (15%)
  blocking collectives  11.5 us (9%)
  matrix products  10.7 us (9%)
    unnamed x3, other arithmetic  26.7 us
    ppermute x6, starting transfers between devices, passed_along(): return lax.ppermute(block, axis, route)  14.6 us
    ppermute x6, waiting for transfers between devices, passed_along(): return lax.ppermute(block, axis, route)  14.5 us
    all_to_all x1, blocking collectives, body(): all_to_all(jnp.stack(jnp.split(xs, axis_size(dev_axis), axis=1), axis=0),...  11.5 us
    unnamed x23, local copies, waits for them, and re-layouts  10.7 us
    dot_general x5, matrix products, fold_block(): jnp.einsum('qgeh,kgh->geqk', q_heads, k_heads, preferred_element_type=jnp...  6.83 us
    dynamic_slice x8, local copies, waits for them, and re-layouts, sweep(): lax.dynamic_index_in_dim(value_window, index, 0, keepdims=False)  4.36 us
    dot_general x5, matrix products, fold_block(): jnp.einsum('geqk,kgh->qgeh', rounded, v_heads, preferred_element_type=jnp...  3.91 us
  transfers between devices with their start and end apart: 9, of which 3 were waited for; matrix products, arithmetic and copies ran while one was open for 34% of the time, Pallas kernels for 0%

profile of v1, /device:TPU:4, one launch (start us, length us, event | category | flops | bytes accessed | tf_op | source)
XLA Modules:
  0.0 124.1 jit_solution(10724036115716719562)
XLA Ops:
  0.0 1.3 %copy.106 = bf16[1,64,1024]{1,0,2:T(2,128)(2,1)S(1)} copy(bf16[1,64,1024]{2,1,0:T(8,128)(2,1)} %param.7) | data formatting | bytes 262144 | tf_op args[1]
  1.3 0.5 broadcast.232
  1.8 2.2 %reduce.1 = bf16[1024,64]{1,0:T(8,128)(2,1)S(1)} reduce(bf16[1024,1,64]{2,1,0:T(2,128)(2,1)S(1)} %bitcast.129, bf16[]{:T(256)} %broadcast.232), dimensions={1}, to_apply=%bitcast.75.reduce_sub_computation | reduce | bytes 262146
  4.0 0.9 reshape.236
  4.8 3.3 %all-to-all-start = ((bf16[4,2,8192]{2,1,0:T(2,128)(2,1)}), bf16[4,2,8192]{2,1,0:T(2,128)(2,1)S(1)}, u32[]{:S(2)}, u32[]{:S(2)}) async-start(bf16[4,2,8192]{2,1,0:T(2,128)(2,1)} %reshape.236), calls=%async_computation | async-start | bytes 262144 | tf_op jit(solution)/shard_map/all_to_all | solution.py:55
  8.2 2.8 %copy.109 = bf16[1,64,4096]{1,0,2:T(2,128)(2,1)S(1)} copy(bf16[1,64,4096]{2,1,0:T(8,128)(2,1)S(1)} %copy-done) | data formatting | bytes 1048576 | tf_op args[0]
  11.0 22.4 %reduce = bf16[4096,64]{1,0:T(8,128)(2,1)S(1)} reduce(bf16[4096,1,64]{2,1,0:T(2,128)(2,1)S(1)} %bitcast.124, bf16[]{:T(256)} %broadcast.232), dimensions={1}, to_apply=%bitcast.77.reduce_sub_computation | reduce | bytes 1048578
  33.4 1.6 %reshape.238 = bf16[4,2,32768]{2,1,0:T(2,128)(2,1)} reshape(bf16[4096,64]{1,0:T(8,128)(2,1)S(1)} %reduce) | data formatting | bytes 1048576
  34.9 0.4 copy.114
  35.3 2.2 %reduce.2 = bf16[1024,64]{1,0:T(8,128)(2,1)S(1)} reduce(bf16[1024,1,64]{2,1,0:T(2,128)(2,1)S(1)} %bitcast.130, bf16[]{:T(256)} %broadcast.232), dimensions={1}, to_apply=%bitcast.79.reduce_sub_computation | reduce | bytes 262146
  37.5 0.9 reshape.240
  38.4 0.2 broadcast_in_dim.114
  38.7 3.3 %all-to-all-start.2 = ((bf16[4,2,8192]{2,1,0:T(2,128)(2,1)}), bf16[4,2,8192]{2,1,0:T(2,128)(2,1)S(1)}, u32[]{:S(2)}, u32[]{:S(2)}) async-start(bf16[4,2,8192]{2,1,0:T(2,128)(2,1)} %reshape.240), calls=%async_computation.2 | async-start | bytes 262144 | tf_op jit(solution)/shard_map/all_to_all | solution.py:56
  42.0 0.3 reshape.237
  42.4 0.3 copy.107
  42.8 3.8 %all-to-all-done.2 = bf16[4,2,8192]{2,1,0:T(2,128)(2,1)S(1)} async-done(((bf16[4,2,8192]{2,1,0:T(2,128)(2,1)}), bf16[4,2,8192]{2,1,0:T(2,128)(2,1)S(1)}, u32[]{:S(2)}, u32[]{:S(2)}) %all-to-all-start.2) | async-done | bytes 131104 | tf_op jit(solution)/shard_map/all_to_all | solution.py:56
  46.6 3.5 %all-to-all-start.1 = ((bf16[4,2,32768]{2,1,0:T(2,128)(2,1)}), bf16[4,2,32768]{2,1,0:T(2,128)(2,1)S(1)}, u32[]{:S(2)}, u32[]{:S(2)}) async-start(bf16[4,2,32768]{2,1,0:T(2,128)(2,1)} %reshape.238), calls=%async_computation.1 | async-start | bytes 1048576 | tf_op jit(solution)/shard_map/all_to_all | solution.py:54
  50.1 0.3 reshape.241
  50.4 0.3 copy.115
  50.8 3.5 %collective-permute-start.1 = (bf16[1,256,256]{2,1,0:T(8,128)(2,1)S(1)}, bf16[1,256,256]{2,1,0:T(8,128)(2,1)S(1)}, u32[]{:S(2)}, u32[]{:S(2)}) collective-permute-start(bf16[1,256,256]{2,1,0:T(8,128)(2,1)S(1)} %bitcast.133), channel_id=1, source_target_pairs={{0,1},{1,2},{2,3},{3,4},{4,5},{5,6},{6,7},{8,9},{9,10},{10,11},{11... | collective-permute-start | bytes 393224 | tf_op jit(solution)/shard_map/ppermute | solution.py:16
  54.3 3.5 %collective-permute-start.4 = (bf16[1,256,256]{2,1,0:T(8,128)(2,1)S(1)}, bf16[1,256,256]{2,1,0:T(8,128)(2,1)S(1)}, u32[]{:S(2)}, u32[]{:S(2)}) collective-permute-start(bf16[1,256,256]{2,1,0:T(8,128)(2,1)S(1)} %bitcast.137), channel_id=1, source_target_pairs={{0,1},{1,2},{2,3},{3,4},{4,5},{5,6},{6,7},{8,9},{9,10},{10,11},{11... | collective-permute-start | bytes 393224 | tf_op jit(solution)/shard_map/ppermute | solution.py:16
  58.0 0.7 reshape_squeeze.11
  58.7 1.3 %collective-permute-start = (bf16[1,256,256]{2,1,0:T(8,128)(2,1)S(1)}, bf16[1,256,256]{2,1,0:T(8,128)(2,1)}, u32[]{:S(2)}, u32[]{:S(2)}) collective-permute-start(bf16[1,256,256]{2,1,0:T(8,128)(2,1)S(1)} %bitcast.134), channel_id=1, source_target_pairs={{0,4},{1,5},{2,6},{3,7},{8,12},{9,13},{10,14},{11,15},{16,20},{17,... | collective-permute-start | bytes 393224 | tf_op jit(solution)/shard_map/ppermute | solution.py:16
  60.0 1.3 %collective-permute-start.3 = (bf16[1,256,256]{2,1,0:T(8,128)(2,1)S(1)}, bf16[1,256,256]{2,1,0:T(8,128)(2,1)S(1)}, u32[]{:S(2)}, u32[]{:S(2)}) collective-permute-start(bf16[1,256,256]{2,1,0:T(8,128)(2,1)S(1)} %bitcast.138), channel_id=1, source_target_pairs={{0,4},{1,5},{2,6},{3,7},{8,12},{9,13},{10,14},{11,15},{16,20},{17,... | collective-permute-start | bytes 393224 | tf_op jit(solution)/shard_map/ppermute | solution.py:16
  61.3 0.7 pad_maximum_fusion.3
  62.1 3.1 %collective-permute-start.2 = (bf16[2,256,256]{2,1,0:T(8,128)(2,1)}, bf16[2,256,256]{2,1,0:T(8,128)(2,1)}, u32[]{:S(2)}, u32[]{:S(2)}) collective-permute-start(bf16[2,256,256]{2,1,0:T(8,128)(2,1)} %pad_maximum_fusion.3), channel_id=1, source_target_pairs={{0,2},{1,3},{2,4},{3,5},{4,6},{5,7},{8,10},{9,11},{10,12},{11,13},... | collective-permute-start | bytes 786440 | tf_op jit(solution)/shard_map/ppermute | solution.py:16
  65.2 0.7 pad_maximum_fusion.4
  65.9 1.9 %collective-permute-start.5 = (bf16[2,256,256]{2,1,0:T(8,128)(2,1)}, bf16[2,256,256]{2,1,0:T(8,128)(2,1)}, u32[]{:S(2)}, u32[]{:S(2)}) collective-permute-start(bf16[2,256,256]{2,1,0:T(8,128)(2,1)} %pad_maximum_fusion.4), channel_id=1, source_target_pairs={{0,2},{1,3},{2,4},{3,5},{4,6},{5,7},{8,10},{9,11},{10,12},{11,13},... | collective-permute-start | bytes 786440 | tf_op jit(solution)/shard_map/ppermute | solution.py:16
  67.8 0.9 reshape.239
  68.7 2.3 %copy.110 = bf16[1,64,4096]{2,1,0:T(8,128)(2,1)S(1)} copy(bf16[1,64,4096]{1,0,2:T(2,128)(2,1)S(1)} %bitcast.123) | data formatting | bytes 1048576 | tf_op jit(solution)/shard_map/all_to_all | solution.py:54
  71.0 0.4 all_to_all.44
  71.6 0.4 reshape_squeeze.10
  71.9 0.5 fusion.16
  72.5 0.5 fusion.20
  73.0 0.8 fusion.21
  73.8 0.9 copy.113
  74.7 0.3 copy.121
  75.0 11.6 %collective-permute-done.2 = bf16[2,256,256]{2,1,0:T(8,128)(2,1)} collective-permute-done((bf16[2,256,256]{2,1,0:T(8,128)(2,1)}, bf16[2,256,256]{2,1,0:T(8,128)(2,1)}, u32[]{:S(2)}, u32[]{:S(2)}) %collective-permute-start.2) | collective-permute-done | bytes 262176 | tf_op jit(solution)/shard_map/ppermute | solution.py:16
  86.6 1.9 %pad_maximum_fusion = bf16[5,256,256]{2,1,0:T(8,128)(2,1)} fusion(bf16[1,256,256]{2,1,0:T(8,128)(2,1)S(1)} %bitcast.136, bf16[1,256,256]{2,1,0:T(8,128)(2,1)S(1)} %collective-permute-done.1, bf16[2,256,256]{2,1,0:T(8,128)(2,1)} %collective-permute-done.2, bf16[1,256,256]{2,1,0:T(8,128)(2,1)} %collective-permute-done), kind=kLoop, calls=%fused_computation.40 | loop fusion | flops 983040 | bytes 1310720 | tf_op jit(solution)/shard_map/concatenate | solution.py:85
  88.5 2.9 %collective-permute-done.5 = bf16[2,256,256]{2,1,0:T(8,128)(2,1)} collective-permute-done((bf16[2,256,256]{2,1,0:T(8,128)(2,1)}, bf16[2,256,256]{2,1,0:T(8,128)(2,1)}, u32[]{:S(2)}, u32[]{:S(2)}) %collective-permute-start.5) | collective-permute-done | bytes 262176 | tf_op jit(solution)/shard_map/ppermute | solution.py:16
  91.4 1.9 %pad_maximum_fusion.1 = bf16[5,256,256]{2,1,0:T(8,128)(2,1)} fusion(bf16[1,256,256]{2,1,0:T(8,128)(2,1)S(1)} %bitcast.140, bf16[1,256,256]{2,1,0:T(8,128)(2,1)S(1)} %collective-permute-done.4, bf16[2,256,256]{2,1,0:T(8,128)(2,1)} %collective-permute-done.5, bf16[1,256,256]{2,1,0:T(8,128)(2,1)S(1)} %collective-permute-done.3), kind=kLoop, calls=%fused_computation.41 | loop fusion | flops 983040 | bytes 1310720 | tf_op jit(solution)/shard_map/concatenate | solution.py:86
  93.3 17.5 %while.20 = (s32[]{:T(128)}, f32[2,4,256]{2,1,0:T(4,128)S(1)}, f32[2,4,256]{2,1,0:T(4,128)S(1)}, f32[256,2,4,128]{0,3,2,1:T(8,128)S(1)}, s32[]{:T(128)}, /*index...) while((s32[]{:T(128)}, f32[2,4,256]{2,1,0:T(4,128)S(1)}, ...), condition=%wide.region_8.9_spmd.clone, body=%wide.region_4.0_spmd.clone.sunk | while | flops 274999040 | bytes 10625787 | solution.py:95
  93.6 1.0 constant_dynamic-slice_fusion.3
  94.7 1.6 %fusion.51 = (f32[2,4,256]{2,1,0:T(4,128)S(1)}, f32[2,256,256,4]{2,1,3,0:T(8,128)S(1)}) fusion(pred[256,256]{0,1:T(8,128)(4,1)S(1)} %compare_and_fusion.3, bf16[256,2,128,1]{0,2,3,1:T(8,128)(2,1)S(1)} %bitcast.121, bf16[256,2,4,128]{3,0,2,1:T(8,128)(2,1)} %get-tuple-element.537), kind=kOutput, calls=%fused_computation.3.clone.1 | convolution fusion | flops 135788544 | bytes 2826240 | tf_op jit(solution)/shard_map/while/body/eval_jaxpr/qgeh,kgh->geqk/dot_general | solution.py:37
  96.4 0.8 fusion.54
  97.2 0.5 fusion.53
  97.8 0.2 compare_and_fusion.3
  98.0 1.0 constant_dynamic-slice_fusion.3
  99.1 1.6 %fusion.51 = (f32[2,4,256]{2,1,0:T(4,128)S(1)}, f32[2,256,256,4]{2,1,3,0:T(8,128)S(1)}) fusion(pred[256,256]{0,1:T(8,128)(4,1)S(1)} %compare_and_fusion.3, bf16[256,2,128,1]{0,2,3,1:T(8,128)(2,1)S(1)} %bitcast.121, bf16[256,2,4,128]{3,0,2,1:T(8,128)(2,1)} %get-tuple-element.537), kind=kOutput, calls=%fused_computation.3.clone.1 | convolution fusion | flops 135788544 | bytes 2826240 | tf_op jit(solution)/shard_map/while/body/eval_jaxpr/qgeh,kgh->geqk/dot_general | solution.py:37
  100.8 0.8 fusion.54
  101.5 0.5 fusion.53
  102.1 0.2 compare_and_fusion.3
  102.3 1.0 constant_dynamic-slice_fusion.3
  103.4 1.6 %fusion.51 = (f32[2,4,256]{2,1,0:T(4,128)S(1)}, f32[2,256,256,4]{2,1,3,0:T(8,128)S(1)}) fusion(pred[256,256]{0,1:T(8,128)(4,1)S(1)} %compare_and_fusion.3, bf16[256,2,128,1]{0,2,3,1:T(8,128)(2,1)S(1)} %bitcast.121, bf16[256,2,4,128]{3,0,2,1:T(8,128)(2,1)} %get-tuple-element.537), kind=kOutput, calls=%fused_computation.3.clone.1 | convolution fusion | flops 135788544 | bytes 2826240 | tf_op jit(solution)/shard_map/while/body/eval_jaxpr/qgeh,kgh->geqk/dot_general | solution.py:37
  105.1 0.8 fusion.54
  105.9 0.5 fusion.53
  106.5 0.2 compare_and_fusion.3
  106.7 1.0 constant_dynamic-slice_fusion.3
  107.8 1.6 %fusion.51 = (f32[2,4,256]{2,1,0:T(4,128)S(1)}, f32[2,256,256,4]{2,1,3,0:T(8,128)S(1)}) fusion(pred[256,256]{0,1:T(8,128)(4,1)S(1)} %compare_and_fusion.3, bf16[256,2,128,1]{0,2,3,1:T(8,128)(2,1)S(1)} %bitcast.121, bf16[256,2,4,128]{3,0,2,1:T(8,128)(2,1)} %get-tuple-element.537), kind=kOutput, calls=%fused_computation.3.clone.1 | convolution fusion | flops 135788544 | bytes 2826240 | tf_op jit(solution)/shard_map/while/body/eval_jaxpr/qgeh,kgh->geqk/dot_general | solution.py:37
  109.5 0.8 fusion.54
  110.3 0.5 fusion.53
  110.9 0.2 fusion.35
  111.7 11.5 %all_to_all.56 = bf16[4,1,64,1024]{3,2,1,0:T(8,128)(2,1)S(1)} all-to-all(bf16[4,1,64,1024]{3,2,1,0:T(8,128)(2,1)S(1)} %pad_maximum_fusion.2), channel_id=1, replica_groups=mesh['head'=4,'outer'=2,'inner'=4] {'head'}, dimensions={0} | all-to-all | bytes 1048576 | tf_op jit(solution)/shard_map/all_to_all | solution.py:100
  123.3 0.8 copy.146
  (65 shorter events, 2.8 us)
Async XLA Ops:
  0.0 8.2 %copy-start = (bf16[1,64,4096]{2,1,0:T(8,128)(2,1)S(1)}, bf16[1,64,4096]{2,1,0:T(8,128)(2,1)}, u32[]{:S(2)}) copy-start(bf16[1,64,4096]{2,1,0:T(8,128)(2,1)} %param.6) | copy-start | bytes 1572868
  4.8 33.8 %all-to-all-start = ((bf16[4,2,8192]{2,1,0:T(2,128)(2,1)}), bf16[4,2,8192]{2,1,0:T(2,128)(2,1)S(1)}, u32[]{:S(2)}, u32[]{:S(2)}) async-start(bf16[4,2,8192]{2,1,0:T(2,128)(2,1)} %reshape.236), calls=%async_computation | async-start | bytes 262144 | tf_op jit(solution)/shard_map/all_to_all | solution.py:55
  11.0 23.9 %copy-start.1 = (bf16[1,64,1024]{2,1,0:T(8,128)(2,1)S(1)}, bf16[1,64,1024]{2,1,0:T(8,128)(2,1)}, u32[]{:S(2)}) copy-start(bf16[1,64,1024]{2,1,0:T(8,128)(2,1)} %param.8) | copy-start | bytes 393220
  33.4 5.0 %copy-start.3 = (s32[4]{0:T(128)S(1)}, s32[4]{0:T(128)}, u32[]{:S(2)}) copy-start(s32[4]{0:T(128)} %param.9) | copy-start | bytes 52
  38.7 7.9 %all-to-all-start.2 = ((bf16[4,2,8192]{2,1,0:T(2,128)(2,1)}), bf16[4,2,8192]{2,1,0:T(2,128)(2,1)S(1)}, u32[]{:S(2)}, u32[]{:S(2)}) async-start(bf16[4,2,8192]{2,1,0:T(2,128)(2,1)} %reshape.240), calls=%async_computation.2 | async-start | bytes 262144 | tf_op jit(solution)/shard_map/all_to_all | solution.py:56
  46.6 21.2 %all-to-all-start.1 = ((bf16[4,2,32768]{2,1,0:T(2,128)(2,1)}), bf16[4,2,32768]{2,1,0:T(2,128)(2,1)S(1)}, u32[]{:S(2)}, u32[]{:S(2)}) async-start(bf16[4,2,32768]{2,1,0:T(2,128)(2,1)} %reshape.238), calls=%async_computation.1 | async-start | bytes 1048576 | tf_op jit(solution)/shard_map/all_to_all | solution.py:54
  50.8 10.5 %collective-permute-start.1 = (bf16[1,256,256]{2,1,0:T(8,128)(2,1)S(1)}, bf16[1,256,256]{2,1,0:T(8,128)(2,1)S(1)}, u32[]{:S(2)}, u32[]{:S(2)}) collective-permute-start(bf16[1,256,256]{2,1,0:T(8,128)(2,1)S(1)} %bitcast.133), channel_id=1, source_target_pairs={{0,1},{1,2},{2,3},{3,4},{4,5},{5,6},{6,7},{8,9},{9,10},{10,11},{11... | collective-permute-start | bytes 393224 | tf_op jit(solution)/shard_map/ppermute | solution.py:16
  54.3 10.8 %collective-permute-start.4 = (bf16[1,256,256]{2,1,0:T(8,128)(2,1)S(1)}, bf16[1,256,256]{2,1,0:T(8,128)(2,1)S(1)}, u32[]{:S(2)}, u32[]{:S(2)}) collective-permute-start(bf16[1,256,256]{2,1,0:T(8,128)(2,1)S(1)} %bitcast.137), channel_id=1, source_target_pairs={{0,1},{1,2},{2,3},{3,4},{4,5},{5,6},{6,7},{8,9},{9,10},{10,11},{11... | collective-permute-start | bytes 393224 | tf_op jit(solution)/shard_map/ppermute | solution.py:16
  58.7 16.3 %collective-permute-start = (bf16[1,256,256]{2,1,0:T(8,128)(2,1)S(1)}, bf16[1,256,256]{2,1,0:T(8,128)(2,1)}, u32[]{:S(2)}, u32[]{:S(2)}) collective-permute-start(bf16[1,256,256]{2,1,0:T(8,128)(2,1)S(1)} %bitcast.134), channel_id=1, source_target_pairs={{0,4},{1,5},{2,6},{3,7},{8,12},{9,13},{10,14},{11,15},{16,20},{17,... | collective-permute-start | bytes 393224 | tf_op jit(solution)/shard_map/ppermute | solution.py:16
  60.0 28.5 %collective-permute-start.3 = (bf16[1,256,256]{2,1,0:T(8,128)(2,1)S(1)}, bf16[1,256,256]{2,1,0:T(8,128)(2,1)S(1)}, u32[]{:S(2)}, u32[]{:S(2)}) collective-permute-start(bf16[1,256,256]{2,1,0:T(8,128)(2,1)S(1)} %bitcast.138), channel_id=1, source_target_pairs={{0,4},{1,5},{2,6},{3,7},{8,12},{9,13},{10,14},{11,15},{16,20},{17,... | collective-permute-start | bytes 393224 | tf_op jit(solution)/shard_map/ppermute | solution.py:16
  62.1 24.6 %collective-permute-start.2 = (bf16[2,256,256]{2,1,0:T(8,128)(2,1)}, bf16[2,256,256]{2,1,0:T(8,128)(2,1)}, u32[]{:S(2)}, u32[]{:S(2)}) collective-permute-start(bf16[2,256,256]{2,1,0:T(8,128)(2,1)} %pad_maximum_fusion.3), channel_id=1, source_target_pairs={{0,2},{1,3},{2,4},{3,5},{4,6},{5,7},{8,10},{9,11},{10,12},{11,13},... | collective-permute-start | bytes 786440 | tf_op jit(solution)/shard_map/ppermute | solution.py:16
  65.9 25.5 %collective-permute-start.5 = (bf16[2,256,256]{2,1,0:T(8,128)(2,1)}, bf16[2,256,256]{2,1,0:T(8,128)(2,1)}, u32[]{:S(2)}, u32[]{:S(2)}) collective-permute-start(bf16[2,256,256]{2,1,0:T(8,128)(2,1)} %pad_maximum_fusion.4), channel_id=1, source_target_pairs={{0,2},{1,3},{2,4},{3,5},{4,6},{5,7},{8,10},{9,11},{10,12},{11,13},... | collective-permute-start | bytes 786440 | tf_op jit(solution)/shard_map/ppermute | solution.py:16
  71.9 1.0 copy-start.2
